TPU v7x, 32 devices: a whole 2x2x4 slice. The times are simulated.
32 devices in a mesh: gx: 8 (over z, y), gy: 2 (over x), ha: 2 (over core).
Axes of the slice: x: 2, y: 2, z: 4, core: 2. Of those that a mesh axis runs over, the one named last changes fastest.
Arguments:
- coupling: bfloat16 [8, 4, 4, 768, 768], P('gx', ('gy', 'ha')), may hold values from -0.125 to 0.125
- interior_inverse: bfloat16 [8, 4, 4, 768, 768], P('gx', ('gy', 'ha')), as said below
- boundary_stiffness: bfloat16 [8, 4, 768, 768], P('gx', ('gy', 'ha')), as said below
- block_counts: int32 [8, 4], P('gx', ('gy', 'ha')), may hold values from 1 to 4, as said below
- initial_traces: float32 [8, 4, 768, 128], P('gx', ('gy', 'ha')), may hold values from -2 to 2
- trace_loads: float32 [8, 4, 768, 128], P('gx', ('gy', 'ha')), may hold values from -18 to 18
Outputs:
- traces: float32 [8, 4, 768, 128], P('gx', ('gy', 'ha'))
- residual: float32 [8, 4, 768, 128], P('gx', ('gy', 'ha'))
Inputs may be any that keep to these rules, and one draw needn't show every extreme that they name: `block_counts`: the two cells in columns 2m and 2m+1 of one grid row hold at most 5 blocks together; some cell holds 4. `interior_inverse`: symmetric in its last two dimensions. `boundary_stiffness`: symmetric in its last two dimensions.
All inputs are finite; a program needn't handle non-finite values.
Results may differ from a plain program's by a relative error of at most 0.00095.
Values may be sent and summed in bfloat16 or wider, within the bound.
A program may use at most 128 MiB of HBM per device.

v0:
```python
import functools

import jax
import jax.numpy as jnp
from jax import lax
from jax.experimental import pallas as pl
from jax.experimental.pallas import tpu as pltpu
from jax.sharding import PartitionSpec as P

SWEEPS = 3
FACES = 6

penalty_weight = 2.0
lower_bound = 1.0
upper_bound = 14.0
spectrum_centre = (upper_bound + lower_bound) / 2.0
spectrum_half = (upper_bound - lower_bound) / 2.0
sigma_ratio = spectrum_centre / spectrum_half


def sweep_weights():
    weights = [(0.0, 1.0 / spectrum_centre)]
    weight_old = 1.0 / sigma_ratio
    for _ in range(SWEEPS - 1):
        weight_new = 1.0 / (2.0 * sigma_ratio - weight_old)
        weights.append((weight_new * weight_old, 2.0 * weight_new / spectrum_half))
        weight_old = weight_new
    return weights


def two_parts(value):
    high = value.astype(jnp.bfloat16)
    low = (value - high.astype(jnp.float32)).astype(jnp.bfloat16)
    return high, low


def product(left, right, dims):
    return lax.dot_general(left, right, (dims, ((), ())), preferred_element_type=jnp.float32)


def kernel(
    axis_sizes,
    coupling,
    inverse,
    stiffness,
    counts,
    initial,
    loads,
    traces_out,
    residual_out,
    wide,
    inv,
    factors,
    turned,
    inner,
    held,
    bound,
    direction,
    landed,
    in_sems,
    send_sems,
    recv_sems,
):
    slots, trace_width, inner_width = coupling.shape
    load_width = initial.shape[1]
    mode_width = trace_width // FACES
    rows, groups, halves = axis_sizes
    columns = groups * halves
    row = lax.axis_index("gx")
    column = lax.axis_index("gy") * halves + lax.axis_index("ha")

    def column_id(index):
        return {"gy": lax.div(index, halves), "ha": lax.rem(index, halves)}

    routes = (
        (1, 0, row + 1 < rows, {"gx": row + 1}),
        (0, 1, row > 0, {"gx": row - 1}),
        (3, 2, column + 1 < columns, column_id(column + 1)),
        (2, 3, column > 0, column_id(column - 1)),
    )
    arrivals = ((0, row > 0), (1, row + 1 < rows), (2, column > 0), (3, column + 1 < columns))

    copies = [
        pltpu.make_async_copy(initial, held, in_sems.at[0]),
        pltpu.make_async_copy(loads, bound, in_sems.at[1]),
        pltpu.make_async_copy(stiffness, wide.at[:, pl.ds(0, trace_width)], in_sems.at[2]),
    ]
    coupling_copies, inverse_copies = [], []
    for slot in range(slots):
        spot = pl.ds(trace_width + slot * inner_width, inner_width)
        coupling_copies.append(
            pltpu.make_async_copy(coupling.at[slot], wide.at[:, spot], in_sems.at[3 + slot])
        )
        inverse_copies.append(
            pltpu.make_async_copy(inverse.at[slot], inv.at[slot], in_sems.at[3 + slots + slot])
        )
    copies[0].start()
    for copy in coupling_copies + inverse_copies:
        copy.start()
    copies[2].start()
    copies[1].start()

    barrier = pltpu.get_barrier_semaphore()
    partners = 0
    for _, _, exists, target in routes:
        partners = partners + exists.astype(jnp.int32)

        @pl.when(exists)
        def _():
            pl.semaphore_signal(barrier, inc=1, device_id=target, device_id_type=pl.DeviceIdType.MESH)

    for face, exists in arrivals:

        @pl.when(jnp.logical_not(exists))
        def _():
            landed[:, face] = jnp.zeros((SWEEPS + 1, mode_width, load_width), jnp.float32)

    pl.semaphore_wait(barrier, partners)

    def outgoing(step, route):
        face, spot, _, target = route
        return pltpu.make_async_remote_copy(
            src_ref=held.at[pl.ds(face * mode_width, mode_width)],
            dst_ref=landed.at[step, spot],
            send_sem=send_sems.at[face],
            recv_sem=recv_sems.at[step, spot],
            device_id=target,
            device_id_type=pl.DeviceIdType.MESH,
        )

    def send(step, route):
        @pl.when(route[2])
        def _():
            outgoing(step, route).start()

    def wait_sent(step):
        for route in routes:

            @pl.when(route[2])
            def _():
                outgoing(step, route).wait_send()

    def wait_arrived(step):
        for (face, exists), route in zip(arrivals, routes):

            @pl.when(exists)
            def _():
                outgoing(step, route).wait_recv()

    def keep_parts(traces):
        high, low = two_parts(traces)
        factors[pl.ds(0, trace_width), pl.ds(0, load_width)] = high
        factors[pl.ds(0, trace_width), pl.ds(load_width, load_width)] = low
        high, low = two_parts(traces.T)
        turned[pl.ds(0, load_width)] = high
        turned[pl.ds(load_width, load_width)] = low

    def apply(first):
        @pl.when(first)
        def _():
            for copy in coupling_copies:
                copy.wait()

        for slot in range(slots):
            spot = pl.ds(trace_width + slot * inner_width, inner_width)
            both = product(turned[...], wide[:, spot], ((1,), (0,)))
            high, low = two_parts(both[:load_width] + both[load_width:])
            inner[slot, pl.ds(0, load_width)] = high
            inner[slot, pl.ds(load_width, load_width)] = low

        @pl.when(first)
        def _():
            for copy in inverse_copies + copies[1:]:
                copy.wait()

        for slot in range(slots):
            spot = pl.ds(trace_width + slot * inner_width, inner_width)
            both = product(inv[slot], inner[slot], ((1,), (1,)))
            high, low = two_parts((both[:, :load_width] + both[:, load_width:]) * jnp.where(counts[0, 0] > slot, -1.0, 0.0))
            factors[spot, pl.ds(0, load_width)] = high
            factors[spot, pl.ds(load_width, load_width)] = low
        both = product(wide[...], factors[...], ((1,), (0,)))
        return both[:, :load_width] + both[:, load_width:]

    def residual_of(step, coupled):
        residual_out[...] = bound[...] - coupled - penalty_weight * held[...]
        wait_arrived(step)
        for face in range(4):
            spot = pl.ds(face * mode_width, mode_width)
            residual_out[spot] = residual_out[spot] + penalty_weight * landed[step, face]

    def advance(step, old_weight, new_weight):
        wait_sent(step)
        change = new_weight * residual_out[...] + old_weight * direction[...]
        direction[...] = change
        traces = held[...] + change
        held[...] = traces
        for route in routes:
            send(step + 1, route)
        keep_parts(held[...])

    weights = sweep_weights()

    copies[0].wait()
    for route in routes:
        send(0, route)
    keep_parts(held[...])
    direction[...] = jnp.zeros_like(direction)

    def sweep(step, carry):
        residual_of(step, apply(step == 0))

        @pl.when(step < SWEEPS)
        def _():
            old_weight, new_weight = weights[-1]
            for index in range(SWEEPS - 1):
                old_weight = jnp.where(step == index, weights[index][0], old_weight)
                new_weight = jnp.where(step == index, weights[index][1], new_weight)
            advance(step, old_weight, new_weight)

        return carry

    lax.fori_loop(0, SWEEPS + 1, sweep, 0)
    wait_sent(SWEEPS)
    traces_out[...] = held[...]


def on_device(
    axis_sizes, coupling, interior_inverse, boundary_stiffness, block_counts, initial_traces, trace_loads
):
    slots, trace_width, inner_width = coupling.shape[2:]
    load_width = initial_traces.shape[-1]
    mode_width = trace_width // FACES
    whole = pl.BlockSpec(memory_space=pltpu.HBM)
    out = jax.ShapeDtypeStruct((trace_width, load_width), jnp.float32)
    wide_width = trace_width + slots * inner_width
    traces, residual = pl.pallas_call(
        functools.partial(kernel, axis_sizes),
        out_shape=(out, out),
        in_specs=[whole, whole, whole, pl.BlockSpec(memory_space=pltpu.SMEM), whole, whole],
        out_specs=(pl.BlockSpec(memory_space=pltpu.VMEM),) * 2,
        scratch_shapes=[
            pltpu.VMEM((trace_width, wide_width), jnp.bfloat16),
            pltpu.VMEM((slots, inner_width, inner_width), jnp.bfloat16),
            pltpu.VMEM((wide_width, 2 * load_width), jnp.bfloat16),
            pltpu.VMEM((2 * load_width, trace_width), jnp.bfloat16),
            pltpu.VMEM((slots, 2 * load_width, inner_width), jnp.bfloat16),
            pltpu.VMEM((trace_width, load_width), jnp.float32),
            pltpu.VMEM((trace_width, load_width), jnp.float32),
            pltpu.VMEM((trace_width, load_width), jnp.float32),
            pltpu.VMEM((SWEEPS + 1, 4, mode_width, load_width), jnp.float32),
            pltpu.SemaphoreType.DMA((3 + 2 * slots,)),
            pltpu.SemaphoreType.DMA((4,)),
            pltpu.SemaphoreType.DMA((SWEEPS + 1, 4)),
        ],
        compiler_params=pltpu.CompilerParams(
            collective_id=0, has_side_effects=True, vmem_limit_bytes=67043328
        ),
        name="condense_and_sweep",
    )(
        coupling[0, 0],
        interior_inverse[0, 0],
        boundary_stiffness[0, 0],
        block_counts,
        initial_traces[0, 0],
        trace_loads[0, 0],
    )
    return (traces[None, None], residual[None, None])


def solution(mesh):
    in_specs = (
        P("gx", ("gy", "ha"), None, None, None),
        P("gx", ("gy", "ha"), None, None, None),
        P("gx", ("gy", "ha"), None, None),
        P("gx", ("gy", "ha")),
        P("gx", ("gy", "ha"), None, None),
        P("gx", ("gy", "ha"), None, None),
    )
    out_specs = (P("gx", ("gy", "ha"), None, None), P("gx", ("gy", "ha"), None, None))
    axis_sizes = (mesh.shape["gx"], mesh.shape["gy"], mesh.shape["ha"])
    return jax.shard_map(
        functools.partial(on_device, axis_sizes),
        mesh=mesh, in_specs=in_specs, out_specs=out_specs, check_vma=False,
    )
```

profile of v0, /device:TPU:0, one launch (start us, length us, event | category | flops | bytes accessed | tf_op | source)
XLA Modules:
  0.0 29.5 jit_solution(2529162496017982665)
XLA Ops:
  1.3 24.7 %condense_and_sweep.1 = (f32[768,128]{1,0:T(8,128)}, f32[768,128]{1,0:T(8,128)}) custom-call(bf16[4,768,768]{2,1,0:T(8,128)(2,1)} %bitcast.7, bf16[4,768,768]{2,1,0:T(8,128)(2,1)} %bitcast.8, bf16[768,768]{1,0:T(8,128)(2,1)} %bitcast.9, s32[1,1]{1,0:T(1,128)S(6)} %copy.10.counts, f32[768,128]{1,0:T(8,128)} %bitcast.10, f32[768,128]{1,0:T(8,128)} %bitcast.11), custom_call_target="tpu_custom_call" | custom-call | tf_op jit(solution)/shard_map/condense_and_sweep/pallas_call | solution.py:237
  26.0 1.8 %copy.11 = f32[1,1,768,128]{3,2,1,0:T(8,128)} copy(f32[1,1,768,128]{3,2,1,0:T(8,128)} %bitcast.13) | data formatting | bytes 786432
  27.7 1.8 %copy.12 = f32[1,1,768,128]{3,2,1,0:T(8,128)} copy(f32[1,1,768,128]{3,2,1,0:T(8,128)} %bitcast.12) | data formatting | bytes 786432
where the time goes:
time: 29.7 us; the launch traced here: 29.5 us
  Pallas kernels  24.7 us (83%)
  local copies, waits for them, and re-layouts  3.53 us (12%)
  between operations  1.29 us (4%)
    pallas_call x1, Pallas kernels, on_device(): pl.pallas_call(functools.partial(kernel, axis_sizes), out_shape=(out, out...  24.7 us
    unnamed x2, local copies, waits for them, and re-layouts  3.53 us

commit v1 on v0

v1 whole, which is shorter than its diff:
```python
import functools

import jax
import jax.numpy as jnp
from jax import lax
from jax.experimental import pallas as pl
from jax.experimental.pallas import tpu as pltpu
from jax.sharding import PartitionSpec as P

SWEEPS = 3
FACES = 6
LINKED = 4
BLOCK_FACES = 2

penalty_weight = 2.0
lower_bound = 1.0
upper_bound = 14.0
spectrum_centre = (upper_bound + lower_bound) / 2.0
spectrum_half = (upper_bound - lower_bound) / 2.0
sigma_ratio = spectrum_centre / spectrum_half

guess_slope = 8.0


def sweep_weights():
    weights = [(0.0, 1.0 / spectrum_centre)]
    weight_old = 1.0 / sigma_ratio
    for _ in range(SWEEPS - 1):
        weight_new = 1.0 / (2.0 * sigma_ratio - weight_old)
        weights.append((weight_new * weight_old, 2.0 * weight_new / spectrum_half))
        weight_old = weight_new
    return weights


def two_parts(value):
    high = value.astype(jnp.bfloat16)
    low = (value - high.astype(jnp.float32)).astype(jnp.bfloat16)
    return high, low


def dot_nn(left, right):
    return lax.dot_general(left, right, (((1,), (0,)), ((), ())), preferred_element_type=jnp.float32)


def dot_nt(left, right):
    return lax.dot_general(left, right, (((1,), (1,)), ((), ())), preferred_element_type=jnp.float32)


def kernel(
    axis_sizes,
    coupling,
    inverse,
    stiffness,
    counts,
    initial,
    loads,
    traces_out,
    residual_out,
    wide,
    inv,
    stiff,
    products,
    a_high,
    a_low,
    held,
    bound,
    parts,
    traces,
    bound_t,
    residual,
    direction,
    local,
    near,
    guess,
    sent,
    sent_half,
    landed,
    landed_half,
    in_sems,
    send_sems,
    recv_sems,
):
    slots, trace_width, inner_width = coupling.shape
    load_width = initial.shape[1]
    mode = trace_width // FACES
    block = BLOCK_FACES * mode
    blocks = trace_width // block
    rows, groups, halves = axis_sizes
    columns = groups * halves
    row = lax.axis_index("gx")
    column = lax.axis_index("gy") * halves + lax.axis_index("ha")

    def column_id(index):
        return {"gy": lax.div(index, halves), "ha": lax.rem(index, halves)}

    routes = (
        (0, 1, row > 0, {"gx": row - 1}),
        (1, 0, row + 1 < rows, {"gx": row + 1}),
        (2, 3, column > 0, column_id(column - 1)),
        (3, 2, column + 1 < columns, column_id(column + 1)),
    )

    first_copies = [
        pltpu.make_async_copy(initial, held, in_sems.at[0]),
        pltpu.make_async_copy(loads, bound, in_sems.at[1]),
    ]
    stiff_copy = pltpu.make_async_copy(stiffness, stiff, in_sems.at[2])

    def inner_span(slot):
        return pl.ds(slot * inner_width, inner_width)

    coupling_copies, inverse_copies = [], []
    for slot in range(slots):
        coupling_copies.append(
            pltpu.make_async_copy(coupling.at[slot], wide.at[:, inner_span(slot)], in_sems.at[3 + slot])
        )
        inverse_copies.append(
            pltpu.make_async_copy(inverse.at[slot], inv.at[slot], in_sems.at[3 + slots + slot])
        )
    coupling_copies[0].start()
    inverse_copies[0].start()
    for copy in first_copies:
        copy.start()
    for slot in range(1, slots):
        coupling_copies[slot].start()
        inverse_copies[slot].start()
    stiff_copy.start()

    barrier = pltpu.get_barrier_semaphore()
    partners = 0
    for _, _, exists, target in routes:
        partners = partners + exists.astype(jnp.int32)

        @pl.when(exists)
        def _():
            pl.semaphore_signal(barrier, inc=1, device_id=target, device_id_type=pl.DeviceIdType.MESH)

    for face, _, exists, _ in routes:

        @pl.when(jnp.logical_not(exists))
        def _():
            landed[:, face] = jnp.zeros((2, mode, load_width), jnp.float32)
            landed_half[:, face] = jnp.zeros((2, mode, load_width), jnp.bfloat16)

    def message(step, route, arriving=False):
        face, spot, _, target = route
        if arriving:
            spot = face
        source = (
            initial.at[pl.ds(face * mode, mode)],
            sent.at[face],
            sent_half.at[0, face],
            sent_half.at[1, face],
        )[step]
        place = landed.at[step, spot] if step < 2 else landed_half.at[step - 2, spot]
        return pltpu.make_async_remote_copy(
            src_ref=source,
            dst_ref=place,
            send_sem=send_sems.at[step, face],
            recv_sem=recv_sems.at[step, spot],
            device_id=target,
            device_id_type=pl.DeviceIdType.MESH,
        )

    def send(step, faces):
        for route in routes:
            if route[0] in faces:

                @pl.when(route[2])
                def _():
                    message(step, route).start()

    def wait_arrived(step):
        for route in routes:

            @pl.when(route[2])
            def _():
                message(step, route, True).wait_recv()

    def wait_sent():
        for step in range(SWEEPS + 1):
            for route in routes:

                @pl.when(route[2])
                def _():
                    message(step, route).wait_send()

    def there(face):
        return jnp.where(routes[face][2], 1.0, 0.0)

    def face_span(face):
        return pl.ds(face * mode, mode)

    def block_span(index):
        return pl.ds(index * block, block)

    def block_rows(index):
        return slice(index * block, (index + 1) * block)

    weights = sweep_weights()

    def products_of(index):
        span = block_span(index)
        for slot in range(slots):
            if index == 0:
                coupling_copies[slot].wait()
                inverse_copies[slot].wait()
            value = dot_nn(wide[span, inner_span(slot)], inv[slot])
            value = value * jnp.where(counts[0, 0] > slot, 1.0, 0.0)
            products[span, inner_span(slot)] = value.astype(jnp.bfloat16)

    def condense(index):
        span = block_span(index)
        for other in range(index, blocks):
            place = block_span(other)
            value = stiff[span, place].astype(jnp.float32) - dot_nt(products[span, :], wide[place, :])
            a_high[span, place], a_low[span, place] = two_parts(value)

    def applied(index):
        span = block_span(index)
        after = pl.ds(index * block, trace_width - index * block)
        both = dot_nt(parts[:, after], a_high[span, after])
        rest = dot_nt(parts[pl.ds(0, load_width), after], a_low[span, after])
        if index > 0:
            before = pl.ds(0, index * block)
            both = both + dot_nn(parts[:, before], a_high[before, span])
            rest = rest + dot_nn(parts[pl.ds(0, load_width), before], a_low[before, span])
        return both[:load_width] + both[load_width:] + rest

    def keep_parts(value):
        high, low = two_parts(value)
        parts[pl.ds(0, load_width)] = high
        parts[pl.ds(load_width, load_width)] = low

    for copy in first_copies:
        copy.wait()
    start = held[...].T
    traces[...] = start
    keep_parts(start)
    bound_t[...] = bound[...].T

    products_of(0)
    pl.semaphore_wait(barrier, partners)
    send(0, range(LINKED))
    stiff_copy.wait()

    for index in range(blocks):
        if index > 0:
            products_of(index)
        condense(index)
        span = block_span(index)
        value = bound_t[:, span] - applied(index) - penalty_weight * traces[:, span]
        local[:, span] = value
        faces = [face for face in range(LINKED) if face // BLOCK_FACES == index]
        for face in faces:
            sent[face] = value[:, (face % BLOCK_FACES) * mode : (face % BLOCK_FACES + 1) * mode]
        send(1, faces)

    wait_arrived(0)
    for face in range(FACES):
        span = face_span(face)
        value = local[:, span]
        if face < LINKED:
            value = value + penalty_weight * landed[0, face].T
        residual[:, span] = value
        change = weights[0][1] * value
        direction[:, span] = change
    keep_parts(direction[...])

    for index in range(blocks):
        span = block_span(index)
        value = residual[:, span] - applied(index) - penalty_weight * direction[:, span]
        local[:, span] = value
        faces = [face for face in range(LINKED) if face // BLOCK_FACES == index]
        for face in faces:
            sent_half[0, face] = value[
                :, (face % BLOCK_FACES) * mode : (face % BLOCK_FACES + 1) * mode
            ].astype(jnp.bfloat16)
        send(2, faces)

    wait_arrived(1)
    for face in range(FACES):
        span = face_span(face)
        value = local[:, span]
        own = traces[:, span]
        old = direction[:, span]
        if face < LINKED:
            beyond = (weights[0][1] * there(face)) * (landed[1, face] + penalty_weight * own)
            near[0, face] = beyond
            value = value + penalty_weight * beyond
            view = sent_half[0, face].astype(jnp.float32) + penalty_weight * beyond
            view_change = weights[1][0] * old + weights[1][1] * view
            guess[face] = view - guess_slope * view_change
        change = weights[1][0] * old + weights[1][1] * value
        residual[:, span] = value
        near[1, face] = change
        traces[:, span] = own + old + change
    for face in range(FACES):
        span = face_span(face)
        high, low = two_parts(near[1, face])
        parts[pl.ds(0, load_width), span] = high
        parts[pl.ds(load_width, load_width), span] = low

    for index in range(blocks):
        value = applied(index)
        for face in range(index * BLOCK_FACES, (index + 1) * BLOCK_FACES):
            span = face_span(face)
            lane = (face % BLOCK_FACES) * mode
            mine = residual[:, span] - value[:, lane : lane + mode] - penalty_weight * near[1, face]
            local[:, span] = mine
            if face < LINKED:
                sent_half[1, face] = (mine - guess[face]).astype(jnp.bfloat16)
        send(3, [face for face in range(LINKED) if face // BLOCK_FACES == index])

    wait_arrived(2)
    for face in range(FACES):
        span = face_span(face)
        value = local[:, span]
        old = near[1, face]
        if face < LINKED:
            view = landed_half[0, face].astype(jnp.float32) + penalty_weight * direction[:, span]
            beyond = there(face) * (weights[1][0] * near[0, face] + weights[1][1] * view)
            value = value + penalty_weight * beyond
            near[0, face] = beyond
            landed[1, face] = view - guess_slope * beyond + penalty_weight * old
        change = weights[2][0] * old + weights[2][1] * value
        residual[:, span] = value
        direction[:, span] = change
        traces[:, span] = traces[:, span] + change
    keep_parts(direction[...])

    for index in range(blocks):
        span = block_span(index)
        value = residual[:, span] - applied(index) - penalty_weight * direction[:, span]
        residual_out[span] = value.T
    traces_out[...] = traces[...].T

    wait_arrived(3)
    for face in range(LINKED):
        span = face_span(face)
        view = landed[1, face] + landed_half[1, face].astype(jnp.float32)
        beyond = weights[2][0] * near[0, face] + weights[2][1] * view
        beyond = (penalty_weight * there(face)) * beyond
        residual_out[span] = residual_out[span] + beyond.T
    wait_sent()


def write_kernel(traces, residual, traces_out, residual_out, sems):
    copies = [
        pltpu.make_async_copy(traces, traces_out, sems.at[0]),
        pltpu.make_async_copy(residual, residual_out, sems.at[1]),
    ]
    for copy in copies:
        copy.start()
    for copy in copies:
        copy.wait()


def in_hbm(value):
    return pltpu.with_memory_space_constraint(value, pltpu.HBM)


def on_device(
    axis_sizes, coupling, interior_inverse, boundary_stiffness, block_counts, initial_traces, trace_loads
):
    slots, trace_width, inner_width = coupling.shape[2:]
    load_width = initial_traces.shape[-1]
    mode = trace_width // FACES
    whole = pl.BlockSpec(memory_space=pltpu.HBM)
    vmem = pl.BlockSpec(memory_space=pltpu.VMEM)
    out = pltpu.VMEM((trace_width, load_width), jnp.float32)
    tall = pltpu.VMEM((trace_width, load_width), jnp.float32)
    flat = pltpu.VMEM((load_width, trace_width), jnp.float32)
    square = pltpu.VMEM((trace_width, trace_width), jnp.bfloat16)
    long = pltpu.VMEM((trace_width, slots * inner_width), jnp.bfloat16)
    traces, residual = pl.pallas_call(
        functools.partial(kernel, axis_sizes),
        out_shape=(out, out),
        in_specs=[whole, whole, whole, pl.BlockSpec(memory_space=pltpu.SMEM), whole, whole],
        out_specs=(vmem, vmem),
        scratch_shapes=[
            long,
            pltpu.VMEM((slots, inner_width, inner_width), jnp.bfloat16),
            square,
            long,
            square,
            square,
            tall,
            tall,
            pltpu.VMEM((2 * load_width, trace_width), jnp.bfloat16),
            flat,
            flat,
            flat,
            flat,
            flat,
            pltpu.VMEM((2, FACES, load_width, mode), jnp.float32),
            pltpu.VMEM((LINKED, load_width, mode), jnp.float32),
            pltpu.VMEM((LINKED, load_width, mode), jnp.float32),
            pltpu.VMEM((2, LINKED, load_width, mode), jnp.bfloat16),
            pltpu.VMEM((2, LINKED, load_width, mode), jnp.float32),
            pltpu.VMEM((2, LINKED, load_width, mode), jnp.bfloat16),
            pltpu.SemaphoreType.DMA((3 + 2 * slots,)),
            pltpu.SemaphoreType.DMA((SWEEPS + 1, LINKED)),
            pltpu.SemaphoreType.DMA((SWEEPS + 1, LINKED)),
        ],
        compiler_params=pltpu.CompilerParams(
            collective_id=0, has_side_effects=True, vmem_limit_bytes=48 << 20
        ),
        name="condense_and_sweep",
    )(
        in_hbm(coupling[0, 0]),
        in_hbm(interior_inverse[0, 0]),
        in_hbm(boundary_stiffness[0, 0]),
        block_counts,
        in_hbm(initial_traces[0, 0]),
        in_hbm(trace_loads[0, 0]),
    )
    result = jax.ShapeDtypeStruct((trace_width, load_width), jnp.float32)
    traces, residual = pl.pallas_call(
        write_kernel,
        out_shape=(result, result),
        in_specs=[vmem, vmem],
        out_specs=(whole, whole),
        scratch_shapes=[pltpu.SemaphoreType.DMA((2,))],
        name="write_results",
    )(
        pltpu.with_memory_space_constraint(traces, pltpu.VMEM),
        pltpu.with_memory_space_constraint(residual, pltpu.VMEM),
    )
    return (traces[None, None], residual[None, None])


def solution(mesh):
    in_specs = (
        P("gx", ("gy", "ha"), None, None, None),
        P("gx", ("gy", "ha"), None, None, None),
        P("gx", ("gy", "ha"), None, None),
        P("gx", ("gy", "ha")),
        P("gx", ("gy", "ha"), None, None),
        P("gx", ("gy", "ha"), None, None),
    )
    out_specs = (P("gx", ("gy", "ha"), None, None), P("gx", ("gy", "ha"), None, None))
    axis_sizes = (mesh.shape["gx"], mesh.shape["gy"], mesh.shape["ha"])
    return jax.shard_map(
        functools.partial(on_device, axis_sizes),
        mesh=mesh, in_specs=in_specs, out_specs=out_specs, check_vma=False,
    )
```

time: 29.7 us -> 21.9 us (0.74)
  Pallas kernels: 24.7 us -> 20.4 us
  local copies, waits for them, and re-layouts: 3.53 us -> 0 us
    pallas_call x1, Pallas kernels: 24.7 us -> 19.5 us  [on_device(): pl.pallas_call(functools.partial(kernel, axis_sizes), out_shape=(out, out...]
    unnamed x2 -> x0, local copies, waits for them, and re-layouts: 3.53 us -> none
    pallas_call x0 -> x1, Pallas kernels: none -> 0.89 us  [on_device(): pl.pallas_call(write_kernel, out_shape=(result, result), in_specs=[vmem,...]
where the time goes in v1:
time: 21.9 us; the launch traced here: 21.7 us
  Pallas kernels  20.4 us (93%)
  between operations  1.28 us (6%)
    pallas_call x1, Pallas kernels, on_device(): pl.pallas_call(functools.partial(kernel, axis_sizes), out_shape=(out, out...  19.5 us
    pallas_call x1, Pallas kernels, on_device(): pl.pallas_call(write_kernel, out_shape=(result, result), in_specs=[vmem,...  0.89 us

profile of v1, /device:TPU:0, one launch (start us, length us, event | category | flops | bytes accessed | tf_op | source)
XLA Modules:
  0.0 21.7 jit_solution(6304520116509783341)
XLA Ops:
  1.3 19.5 %condense_and_sweep.1 = (f32[768,128]{1,0:T(8,128)S(1)}, f32[768,128]{1,0:T(8,128)S(1)}) custom-call(bf16[4,768,768]{2,1,0:T(8,128)(2,1)} %bitcast.7, bf16[4,768,768]{2,1,0:T(8,128)(2,1)} %bitcast.8, bf16[768,768]{1,0:T(8,128)(2,1)} %bitcast.9, s32[1,1]{1,0:T(1,128)S(6)} %copy.8.counts, f32[768,128]{1,0:T(8,128)} %bitcast.10, f32[768,128]{1,0:T(8,128)} %bitcast.11), custom_call_target="tpu_custom_call" | custom-call | tf_op jit(solution)/shard_map/condense_and_sweep/pallas_call | solution.py:376
  20.8 0.9 %write_results.1 = (f32[768,128]{1,0:T(8,128)}, f32[768,128]{1,0:T(8,128)}) custom-call(f32[768,128]{1,0:T(8,128)S(1)} %get-tuple-element.6.traces, f32[768,128]{1,0:T(8,128)S(1)} %get-tuple-element.7.residual), custom_call_target="tpu_custom_call" | custom-call | tf_op jit(solution)/shard_map/write_results/pallas_call | solution.py:419

commit v2 on v1

--- a/solution.py
+++ b/solution.py
@@ -62,8 +62,7 @@
     products,
     a_high,
     a_low,
-    held,
-    bound,
+    given,
     parts,
     traces,
     bound_t,
@@ -76,6 +75,7 @@
     sent_half,
     landed,
     landed_half,
+    total,
     in_sems,
     send_sems,
     recv_sems,
@@ -100,31 +100,24 @@
         (3, 2, column + 1 < columns, column_id(column + 1)),
     )
 
-    first_copies = [
-        pltpu.make_async_copy(initial, held, in_sems.at[0]),
-        pltpu.make_async_copy(loads, bound, in_sems.at[1]),
-    ]
-    stiff_copy = pltpu.make_async_copy(stiffness, stiff, in_sems.at[2])
-
     def inner_span(slot):
         return pl.ds(slot * inner_width, inner_width)
 
-    coupling_copies, inverse_copies = [], []
+    given_sem, slot_sem = in_sems.at[slots], in_sems
+    pltpu.make_async_copy(initial, given.at[0], given_sem).start()
+    pltpu.make_async_copy(loads, given.at[1], given_sem).start()
     for slot in range(slots):
-        coupling_copies.append(
-            pltpu.make_async_copy(coupling.at[slot], wide.at[:, inner_span(slot)], in_sems.at[3 + slot])
-        )
-        inverse_copies.append(
-            pltpu.make_async_copy(inverse.at[slot], inv.at[slot], in_sems.at[3 + slots + slot])
-        )
-    coupling_copies[0].start()
-    inverse_copies[0].start()
-    for copy in first_copies:
-        copy.start()
-    for slot in range(1, slots):
-        coupling_copies[slot].start()
-        inverse_copies[slot].start()
+        pltpu.make_async_copy(coupling.at[slot], wide.at[:, inner_span(slot)], slot_sem.at[slot]).start()
+        pltpu.make_async_copy(inverse.at[slot], inv.at[slot], slot_sem.at[slot]).start()
+    stiff_copy = pltpu.make_async_copy(stiffness, stiff, in_sems.at[slots + 1])
     stiff_copy.start()
+
+    def wait_given():
+        pltpu.make_async_copy(given, given, given_sem).wait()
+
+    def wait_slot(slot):
+        both = inv.at[pl.ds(0, 2)]
+        pltpu.make_async_copy(both, both, slot_sem.at[slot]).wait()
 
     barrier = pltpu.get_barrier_semaphore()
     partners = 0
@@ -142,10 +135,8 @@
             landed[:, face] = jnp.zeros((2, mode, load_width), jnp.float32)
             landed_half[:, face] = jnp.zeros((2, mode, load_width), jnp.bfloat16)
 
-    def message(step, route, arriving=False):
+    def message(step, route):
         face, spot, _, target = route
-        if arriving:
-            spot = face
         source = (
             initial.at[pl.ds(face * mode, mode)],
             sent.at[face],
@@ -156,8 +147,8 @@
         return pltpu.make_async_remote_copy(
             src_ref=source,
             dst_ref=place,
-            send_sem=send_sems.at[step, face],
-            recv_sem=recv_sems.at[step, spot],
+            send_sem=send_sems.at[0],
+            recv_sem=recv_sems.at[step],
             device_id=target,
             device_id_type=pl.DeviceIdType.MESH,
         )
@@ -170,20 +161,20 @@
                 def _():
                     message(step, route).start()
 
+    def wait_bytes(place, per_face, sem):
+        for number in range(1, LINKED + 1):
+
+            @pl.when(partners == number)
+            def _():
+                part = place.at[pl.ds(0, number * per_face)]
+                pltpu.make_async_copy(part, part, sem).wait()
+
     def wait_arrived(step):
-        for route in routes:
-
-            @pl.when(route[2])
-            def _():
-                message(step, route, True).wait_recv()
+        place = landed.at[step] if step < 2 else landed_half.at[step - 2]
+        wait_bytes(place, 1, recv_sems.at[step])
 
     def wait_sent():
-        for step in range(SWEEPS + 1):
-            for route in routes:
-
-                @pl.when(route[2])
-                def _():
-                    message(step, route).wait_send()
+        wait_bytes(near, 3, send_sems.at[0])
 
     def there(face):
         return jnp.where(routes[face][2], 1.0, 0.0)
@@ -199,22 +190,31 @@
 
     weights = sweep_weights()
 
-    def products_of(index):
+    def product_of(index, slot):
         span = block_span(index)
-        for slot in range(slots):
-            if index == 0:
-                coupling_copies[slot].wait()
-                inverse_copies[slot].wait()
-            value = dot_nn(wide[span, inner_span(slot)], inv[slot])
-            value = value * jnp.where(counts[0, 0] > slot, 1.0, 0.0)
-            products[span, inner_span(slot)] = value.astype(jnp.bfloat16)
+        value = dot_nn(wide[span, inner_span(slot)], inv[slot])
+        value = value * jnp.where(counts[0, 0] > slot, 1.0, 0.0)
+        products[span, inner_span(slot)] = value.astype(jnp.bfloat16)
+
+    def keep_condensed(index, other, value):
+        span, place = block_span(index), block_span(other)
+        value = stiff[span, place].astype(jnp.float32) - value
+        a_high[span, place], a_low[span, place] = two_parts(value)
+
+    def condense_first(slot):
+        for other in range(blocks):
+            place = block_span(other)
+            value = dot_nt(products[block_span(0), inner_span(slot)], wide[place, inner_span(slot)])
+            if slot > 0:
+                value = value + total[:, place]
+            if slot + 1 < slots:
+                total[:, place] = value
+            else:
+                keep_condensed(0, other, value)
 
     def condense(index):
-        span = block_span(index)
         for other in range(index, blocks):
-            place = block_span(other)
-            value = stiff[span, place].astype(jnp.float32) - dot_nt(products[span, :], wide[place, :])
-            a_high[span, place], a_low[span, place] = two_parts(value)
+            keep_condensed(index, other, dot_nt(products[block_span(index), :], wide[block_span(other), :]))
 
     def applied(index):
         span = block_span(index)
@@ -232,22 +232,33 @@
         parts[pl.ds(0, load_width)] = high
         parts[pl.ds(load_width, load_width)] = low
 
-    for copy in first_copies:
-        copy.wait()
-    start = held[...].T
+    wait_given()
+    start = given[0].T
     traces[...] = start
     keep_parts(start)
-    bound_t[...] = bound[...].T
-
-    products_of(0)
-    pl.semaphore_wait(barrier, partners)
-    send(0, range(LINKED))
-    stiff_copy.wait()
+    bound_t[...] = given[1].T
+
+    for slot in range(slots):
+        wait_slot(slot)
+        product_of(0, slot)
+        if slot + 1 < slots:
+            product_of(1, slot)
+        if slot < 1:
+            product_of(2, slot)
+        if slot == 1:
+            pl.semaphore_wait(barrier, partners)
+            send(0, range(LINKED))
+        if slot + 1 == slots:
+            stiff_copy.wait()
+        condense_first(slot)
+    product_of(1, slots - 1)
 
     for index in range(blocks):
+        if index > 1:
+            for slot in range(1, slots):
+                product_of(index, slot)
         if index > 0:
-            products_of(index)
-        condense(index)
+            condense(index)
         span = block_span(index)
         value = bound_t[:, span] - applied(index) - penalty_weight * traces[:, span]
         local[:, span] = value
@@ -286,18 +297,18 @@
         old = direction[:, span]
         if face < LINKED:
             beyond = (weights[0][1] * there(face)) * (landed[1, face] + penalty_weight * own)
-            near[0, face] = beyond
+            near[face] = beyond
             value = value + penalty_weight * beyond
             view = sent_half[0, face].astype(jnp.float32) + penalty_weight * beyond
             view_change = weights[1][0] * old + weights[1][1] * view
             guess[face] = view - guess_slope * view_change
         change = weights[1][0] * old + weights[1][1] * value
         residual[:, span] = value
-        near[1, face] = change
+        near[FACES + face] = change
         traces[:, span] = own + old + change
     for face in range(FACES):
         span = face_span(face)
-        high, low = two_parts(near[1, face])
+        high, low = two_parts(near[FACES + face])
         parts[pl.ds(0, load_width), span] = high
         parts[pl.ds(load_width, load_width), span] = low
 
@@ -306,7 +317,7 @@
         for face in range(index * BLOCK_FACES, (index + 1) * BLOCK_FACES):
             span = face_span(face)
             lane = (face % BLOCK_FACES) * mode
-            mine = residual[:, span] - value[:, lane : lane + mode] - penalty_weight * near[1, face]
+            mine = residual[:, span] - value[:, lane : lane + mode] - penalty_weight * near[FACES + face]
             local[:, span] = mine
             if face < LINKED:
                 sent_half[1, face] = (mine - guess[face]).astype(jnp.bfloat16)
@@ -316,12 +327,12 @@
     for face in range(FACES):
         span = face_span(face)
         value = local[:, span]
-        old = near[1, face]
+        old = near[FACES + face]
         if face < LINKED:
             view = landed_half[0, face].astype(jnp.float32) + penalty_weight * direction[:, span]
-            beyond = there(face) * (weights[1][0] * near[0, face] + weights[1][1] * view)
+            beyond = there(face) * (weights[1][0] * near[face] + weights[1][1] * view)
             value = value + penalty_weight * beyond
-            near[0, face] = beyond
+            near[face] = beyond
             landed[1, face] = view - guess_slope * beyond + penalty_weight * old
         change = weights[2][0] * old + weights[2][1] * value
         residual[:, span] = value
@@ -335,14 +346,14 @@
         residual_out[span] = value.T
     traces_out[...] = traces[...].T
 
+    wait_sent()
     wait_arrived(3)
     for face in range(LINKED):
         span = face_span(face)
         view = landed[1, face] + landed_half[1, face].astype(jnp.float32)
-        beyond = weights[2][0] * near[0, face] + weights[2][1] * view
+        beyond = weights[2][0] * near[face] + weights[2][1] * view
         beyond = (penalty_weight * there(face)) * beyond
         residual_out[span] = residual_out[span] + beyond.T
-    wait_sent()
 
 
 def write_kernel(traces, residual, traces_out, residual_out, sems):
@@ -369,7 +380,6 @@
     whole = pl.BlockSpec(memory_space=pltpu.HBM)
     vmem = pl.BlockSpec(memory_space=pltpu.VMEM)
     out = pltpu.VMEM((trace_width, load_width), jnp.float32)
-    tall = pltpu.VMEM((trace_width, load_width), jnp.float32)
     flat = pltpu.VMEM((load_width, trace_width), jnp.float32)
     square = pltpu.VMEM((trace_width, trace_width), jnp.bfloat16)
     long = pltpu.VMEM((trace_width, slots * inner_width), jnp.bfloat16)
@@ -385,23 +395,23 @@
             long,
             square,
             square,
-            tall,
-            tall,
+            pltpu.VMEM((2, trace_width, load_width), jnp.float32),
             pltpu.VMEM((2 * load_width, trace_width), jnp.bfloat16),
             flat,
             flat,
             flat,
             flat,
             flat,
-            pltpu.VMEM((2, FACES, load_width, mode), jnp.float32),
+            pltpu.VMEM((2 * FACES, load_width, mode), jnp.float32),
             pltpu.VMEM((LINKED, load_width, mode), jnp.float32),
             pltpu.VMEM((LINKED, load_width, mode), jnp.float32),
             pltpu.VMEM((2, LINKED, load_width, mode), jnp.bfloat16),
             pltpu.VMEM((2, LINKED, load_width, mode), jnp.float32),
             pltpu.VMEM((2, LINKED, load_width, mode), jnp.bfloat16),
-            pltpu.SemaphoreType.DMA((3 + 2 * slots,)),
-            pltpu.SemaphoreType.DMA((SWEEPS + 1, LINKED)),
-            pltpu.SemaphoreType.DMA((SWEEPS + 1, LINKED)),
+            pltpu.VMEM((BLOCK_FACES * mode, trace_width), jnp.float32),
+            pltpu.SemaphoreType.DMA((slots + 2,)),
+            pltpu.SemaphoreType.DMA((1,)),
+            pltpu.SemaphoreType.DMA((SWEEPS + 1,)),
         ],
         compiler_params=pltpu.CompilerParams(
             collective_id=0, has_side_effects=True, vmem_limit_bytes=48 << 20

time: 21.9 us -> 20.8 us (0.950)
  Pallas kernels: 20.4 us -> 19.3 us
    pallas_call x1, Pallas kernels: 19.5 us -> 18.4 us  [on_device(): pl.pallas_call(functools.partial(kernel, axis_sizes), out_shape=(out, out...]
where the time goes in v2:
time: 20.8 us; the launch traced here: 20.6 us
  Pallas kernels  19.3 us (93%)
  between operations  1.28 us (6%)
    pallas_call x1, Pallas kernels, on_device(): pl.pallas_call(functools.partial(kernel, axis_sizes), out_shape=(out, out...  18.4 us
    pallas_call x1, Pallas kernels, on_device(): pl.pallas_call(write_kernel, out_shape=(result, result), in_specs=[vmem,...  0.89 us

profile of v2, /device:TPU:0, one launch (start us, length us, event | category | flops | bytes accessed | tf_op | source)
XLA Modules:
  0.0 20.6 jit_solution(8710732200325859860)
XLA Ops:
  1.3 18.4 %condense_and_sweep.1 = (f32[768,128]{1,0:T(8,128)S(1)}, f32[768,128]{1,0:T(8,128)S(1)}) custom-call(bf16[4,768,768]{2,1,0:T(8,128)(2,1)} %bitcast.7, bf16[4,768,768]{2,1,0:T(8,128)(2,1)} %bitcast.8, bf16[768,768]{1,0:T(8,128)(2,1)} %bitcast.9, s32[1,1]{1,0:T(1,128)S(6)} %copy.8.counts, f32[768,128]{1,0:T(8,128)} %bitcast.10, f32[768,128]{1,0:T(8,128)} %bitcast.11), custom_call_target="tpu_custom_call" | custom-call | tf_op jit(solution)/shard_map/condense_and_sweep/pallas_call | solution.py:386
  19.7 0.9 %write_results.1 = (f32[768,128]{1,0:T(8,128)}, f32[768,128]{1,0:T(8,128)}) custom-call(f32[768,128]{1,0:T(8,128)S(1)} %get-tuple-element.6.traces, f32[768,128]{1,0:T(8,128)S(1)} %get-tuple-element.7.residual), custom_call_target="tpu_custom_call" | custom-call | tf_op jit(solution)/shard_map/write_results/pallas_call | solution.py:429

commit v3 on v2

--- a/solution.py
+++ b/solution.py
@@ -11,6 +11,9 @@
 FACES = 6
 LINKED = 4
 BLOCK_FACES = 2
+EARLY = 2
+MEET = 0
+NW = 256
 
 penalty_weight = 2.0
 lower_bound = 1.0
@@ -64,13 +67,13 @@
     a_low,
     given,
     parts,
+    more_parts,
     traces,
     bound_t,
     residual,
     direction,
     local,
     near,
-    guess,
     sent,
     sent_half,
     landed,
@@ -103,21 +106,36 @@
     def inner_span(slot):
         return pl.ds(slot * inner_width, inner_width)
 
-    given_sem, slot_sem = in_sems.at[slots], in_sems
+    def coupling_copy(slot, start, size, sem):
+        rows_of = pl.ds(start, size)
+        pltpu.make_async_copy(coupling.at[slot, rows_of], wide.at[rows_of, inner_span(slot)], sem).start()
+
+    def wait_for(place, sem):
+        pltpu.make_async_copy(place, place, sem).wait()
+
+    chunks = inner_width // block
+    given_sem = in_sems.at[0]
+    chunk_sems = [in_sems.at[1 + chunk] for chunk in range(chunks)]
+    rest_sem, stiff_sem = in_sems.at[1 + chunks], in_sems.at[2 + chunks]
+    slot_sems = [None] + [in_sems.at[2 + chunks + slot] for slot in range(1, slots)]
+    coupling_copy(0, 0, block, chunk_sems[0])
+    for chunk in range(chunks):
+        piece = inv.at[0, pl.ds(chunk * block, block)]
+        pltpu.make_async_copy(inverse.at[0, pl.ds(chunk * block, block)], piece, chunk_sems[chunk]).start()
+    coupling_copy(0, block, trace_width - block, rest_sem)
     pltpu.make_async_copy(initial, given.at[0], given_sem).start()
     pltpu.make_async_copy(loads, given.at[1], given_sem).start()
-    for slot in range(slots):
-        pltpu.make_async_copy(coupling.at[slot], wide.at[:, inner_span(slot)], slot_sem.at[slot]).start()
-        pltpu.make_async_copy(inverse.at[slot], inv.at[slot], slot_sem.at[slot]).start()
-    stiff_copy = pltpu.make_async_copy(stiffness, stiff, in_sems.at[slots + 1])
-    stiff_copy.start()
-
-    def wait_given():
-        pltpu.make_async_copy(given, given, given_sem).wait()
+    def load_slot(slot):
+        coupling_copy(slot, 0, trace_width, slot_sems[slot])
+        pltpu.make_async_copy(inverse.at[slot], inv.at[slot], slot_sems[slot]).start()
+
+    def load_stiff():
+        pltpu.make_async_copy(stiffness, stiff, stiff_sem).start()
+
+    load_slot(1)
 
     def wait_slot(slot):
-        both = inv.at[pl.ds(0, 2)]
-        pltpu.make_async_copy(both, both, slot_sem.at[slot]).wait()
+        wait_for(inv.at[pl.ds(0, 2)], slot_sems[slot])
 
     barrier = pltpu.get_barrier_semaphore()
     partners = 0
@@ -192,7 +210,21 @@
 
     def product_of(index, slot):
         span = block_span(index)
-        value = dot_nn(wide[span, inner_span(slot)], inv[slot])
+        if index == 0 and slot == 0:
+            value = 0.0
+            for chunk in range(chunks):
+                wait_for(inv.at[0, pl.ds(0, block * (2 if chunk == 0 else 1))], chunk_sems[chunk])
+                if chunk == 0:
+                    load_slot(2)
+                inside = pl.ds(chunk * block, block)
+                value = value + dot_nn(wide[span, inside], inv[slot, inside])
+        else:
+            live = jnp.where(counts[0, 0] > slot, 1.0, 0.0)
+            for piece in range(inner_width // NW):
+                inside = pl.ds(piece * NW, NW)
+                value = dot_nn(wide[span, inner_span(slot)], inv[slot, :, inside]) * live
+                products[span, pl.ds(slot * inner_width + piece * NW, NW)] = value.astype(jnp.bfloat16)
+            return
         value = value * jnp.where(counts[0, 0] > slot, 1.0, 0.0)
         products[span, inner_span(slot)] = value.astype(jnp.bfloat16)
 
@@ -216,71 +248,86 @@
         for other in range(index, blocks):
             keep_condensed(index, other, dot_nt(products[block_span(index), :], wide[block_span(other), :]))
 
-    def applied(index):
-        span = block_span(index)
-        after = pl.ds(index * block, trace_width - index * block)
-        both = dot_nt(parts[:, after], a_high[span, after])
-        rest = dot_nt(parts[pl.ds(0, load_width), after], a_low[span, after])
+    def applied(index, source, depth):
+        span = block_span(index)
+        ones = pl.ds(0, load_width)
+        both, rest = [], []
+        if index < depth:
+            after = pl.ds(index * block, (depth - index) * block)
+            both.append(dot_nt(source[:, after], a_high[span, after]))
+            rest.append(dot_nt(source[ones, after], a_low[span, after]))
         if index > 0:
-            before = pl.ds(0, index * block)
-            both = both + dot_nn(parts[:, before], a_high[before, span])
-            rest = rest + dot_nn(parts[pl.ds(0, load_width), before], a_low[before, span])
+            before = pl.ds(0, min(index, depth) * block)
+            both.append(dot_nn(source[:, before], a_high[before, span]))
+            rest.append(dot_nn(source[ones, before], a_low[before, span]))
+        both, rest = sum(both[1:], both[0]), sum(rest[1:], rest[0])
         return both[:load_width] + both[load_width:] + rest
+
+    def keep_face_parts(place, span, value):
+        high, low = two_parts(value)
+        place[pl.ds(0, load_width), span] = high
+        place[pl.ds(load_width, load_width), span] = low
 
     def keep_parts(value):
         high, low = two_parts(value)
         parts[pl.ds(0, load_width)] = high
         parts[pl.ds(load_width, load_width)] = low
 
-    wait_given()
-    start = given[0].T
-    traces[...] = start
-    keep_parts(start)
-    bound_t[...] = given[1].T
-
     for slot in range(slots):
-        wait_slot(slot)
+        if slot > 0:
+            wait_slot(slot)
         product_of(0, slot)
-        if slot + 1 < slots:
+        if slot == 0:
+            wait_for(wide.at[pl.ds(0, trace_width - block), inner_span(0)], rest_sem)
+            load_slot(3)
+            load_stiff()
+        if slot < EARLY:
             product_of(1, slot)
-        if slot < 1:
-            product_of(2, slot)
-        if slot == 1:
+        if slot == 0:
+            wait_for(given, given_sem)
+            start = given[0].T
+            traces[...] = start
+            keep_parts(start)
+            bound_t[...] = given[1].T
+        if slot == MEET:
             pl.semaphore_wait(barrier, partners)
             send(0, range(LINKED))
         if slot + 1 == slots:
-            stiff_copy.wait()
+            wait_for(stiff, stiff_sem)
         condense_first(slot)
-    product_of(1, slots - 1)
-
+
+    linked_blocks = LINKED // BLOCK_FACES
     for index in range(blocks):
-        if index > 1:
-            for slot in range(1, slots):
+        if index > 0:
+            for slot in range(EARLY if index == 1 else 0, slots):
                 product_of(index, slot)
-        if index > 0:
             condense(index)
         span = block_span(index)
-        value = bound_t[:, span] - applied(index) - penalty_weight * traces[:, span]
-        local[:, span] = value
-        faces = [face for face in range(LINKED) if face // BLOCK_FACES == index]
-        for face in faces:
-            sent[face] = value[:, (face % BLOCK_FACES) * mode : (face % BLOCK_FACES + 1) * mode]
-        send(1, faces)
-
-    wait_arrived(0)
-    for face in range(FACES):
-        span = face_span(face)
-        value = local[:, span]
-        if face < LINKED:
-            value = value + penalty_weight * landed[0, face].T
-        residual[:, span] = value
-        change = weights[0][1] * value
-        direction[:, span] = change
-    keep_parts(direction[...])
+        value = bound_t[:, span] - applied(index, parts, blocks) - penalty_weight * traces[:, span]
+        if index < linked_blocks:
+            local[:, span] = value
+            faces = range(index * BLOCK_FACES, (index + 1) * BLOCK_FACES)
+            for face in faces:
+                sent[face] = value[:, (face % BLOCK_FACES) * mode : (face % BLOCK_FACES + 1) * mode]
+            send(1, faces)
+        else:
+            residual[:, span] = value
+            change = weights[0][1] * value
+            direction[:, span] = change
+            keep_face_parts(more_parts, span, change)
+        if index + 1 == linked_blocks:
+            wait_arrived(0)
+            for face in range(LINKED):
+                span = face_span(face)
+                value = local[:, span] + penalty_weight * landed[0, face].T
+                residual[:, span] = value
+                change = weights[0][1] * value
+                direction[:, span] = change
+                keep_face_parts(more_parts, span, change)
 
     for index in range(blocks):
         span = block_span(index)
-        value = residual[:, span] - applied(index) - penalty_weight * direction[:, span]
+        value = residual[:, span] - applied(index, more_parts, blocks) - penalty_weight * direction[:, span]
         local[:, span] = value
         faces = [face for face in range(LINKED) if face // BLOCK_FACES == index]
         for face in faces:
@@ -293,58 +340,66 @@
     for face in range(FACES):
         span = face_span(face)
         value = local[:, span]
-        own = traces[:, span]
-        old = direction[:, span]
         if face < LINKED:
-            beyond = (weights[0][1] * there(face)) * (landed[1, face] + penalty_weight * own)
+            beyond = (weights[0][1] * there(face)) * (landed[1, face] + penalty_weight * traces[:, span])
             near[face] = beyond
             value = value + penalty_weight * beyond
-            view = sent_half[0, face].astype(jnp.float32) + penalty_weight * beyond
-            view_change = weights[1][0] * old + weights[1][1] * view
-            guess[face] = view - guess_slope * view_change
-        change = weights[1][0] * old + weights[1][1] * value
+        change = weights[1][0] * direction[:, span] + weights[1][1] * value
         residual[:, span] = value
         near[FACES + face] = change
-        traces[:, span] = own + old + change
-    for face in range(FACES):
-        span = face_span(face)
-        high, low = two_parts(near[FACES + face])
-        parts[pl.ds(0, load_width), span] = high
-        parts[pl.ds(load_width, load_width), span] = low
+        keep_face_parts(parts, span, change)
 
     for index in range(blocks):
-        value = applied(index)
+        value = applied(index, parts, blocks)
         for face in range(index * BLOCK_FACES, (index + 1) * BLOCK_FACES):
             span = face_span(face)
             lane = (face % BLOCK_FACES) * mode
             mine = residual[:, span] - value[:, lane : lane + mode] - penalty_weight * near[FACES + face]
             local[:, span] = mine
             if face < LINKED:
-                sent_half[1, face] = (mine - guess[face]).astype(jnp.bfloat16)
+                view = sent_half[0, face].astype(jnp.float32) + penalty_weight * near[face]
+                view_change = weights[1][0] * direction[:, span] + weights[1][1] * view
+                sent_half[1, face] = (mine - (view - guess_slope * view_change)).astype(jnp.bfloat16)
         send(3, [face for face in range(LINKED) if face // BLOCK_FACES == index])
-
-    wait_arrived(2)
     for face in range(FACES):
         span = face_span(face)
-        value = local[:, span]
-        old = near[FACES + face]
-        if face < LINKED:
-            view = landed_half[0, face].astype(jnp.float32) + penalty_weight * direction[:, span]
-            beyond = there(face) * (weights[1][0] * near[face] + weights[1][1] * view)
-            value = value + penalty_weight * beyond
-            near[face] = beyond
-            landed[1, face] = view - guess_slope * beyond + penalty_weight * old
-        change = weights[2][0] * old + weights[2][1] * value
-        residual[:, span] = value
-        direction[:, span] = change
-        traces[:, span] = traces[:, span] + change
-    keep_parts(direction[...])
-
+        change = weights[2][0] * near[FACES + face] + weights[2][1] * local[:, span]
+        keep_face_parts(more_parts, span, change)
+        residual[:, span] = local[:, span] - penalty_weight * change
+        traces[:, span] = traces[:, span] + direction[:, span] + near[FACES + face] + change
     for index in range(blocks):
         span = block_span(index)
-        value = residual[:, span] - applied(index) - penalty_weight * direction[:, span]
-        residual_out[span] = value.T
-    traces_out[...] = traces[...].T
+        residual[:, span] = residual[:, span] - applied(index, more_parts, blocks)
+    for index in range(linked_blocks, blocks):
+        span = block_span(index)
+        traces_out[span] = traces[:, span].T
+
+    wait_arrived(2)
+    for face in range(LINKED):
+        span = face_span(face)
+        view = landed_half[0, face].astype(jnp.float32) + penalty_weight * direction[:, span]
+        beyond = there(face) * (weights[1][0] * near[face] + weights[1][1] * view)
+        near[face] = beyond
+        change = (weights[2][1] * penalty_weight) * beyond
+        local[:, span] = change
+        keep_face_parts(parts, span, change)
+
+    for index in range(blocks):
+        span = block_span(index)
+        value = residual[:, span] - applied(index, parts, linked_blocks)
+        if index < linked_blocks:
+            for face in range(index * BLOCK_FACES, (index + 1) * BLOCK_FACES):
+                lane = (face % BLOCK_FACES) * mode
+                change = local[:, face_span(face)]
+                mine = value[:, lane : lane + mode] + penalty_weight * (near[face] - change)
+                residual_out[face_span(face)] = mine.T
+                traces_out[face_span(face)] = (traces[:, face_span(face)] + change).T
+        else:
+            residual_out[span] = value.T
+    for face in range(LINKED):
+        span = face_span(face)
+        view = landed_half[0, face].astype(jnp.float32) + penalty_weight * direction[:, span]
+        landed[1, face] = view - guess_slope * near[face] + penalty_weight * near[FACES + face]
 
     wait_sent()
     wait_arrived(3)
@@ -397,6 +452,7 @@
             square,
             pltpu.VMEM((2, trace_width, load_width), jnp.float32),
             pltpu.VMEM((2 * load_width, trace_width), jnp.bfloat16),
+            pltpu.VMEM((2 * load_width, trace_width), jnp.bfloat16),
             flat,
             flat,
             flat,
@@ -404,12 +460,11 @@
             flat,
             pltpu.VMEM((2 * FACES, load_width, mode), jnp.float32),
             pltpu.VMEM((LINKED, load_width, mode), jnp.float32),
-            pltpu.VMEM((LINKED, load_width, mode), jnp.float32),
             pltpu.VMEM((2, LINKED, load_width, mode), jnp.bfloat16),
             pltpu.VMEM((2, LINKED, load_width, mode), jnp.float32),
             pltpu.VMEM((2, LINKED, load_width, mode), jnp.bfloat16),
             pltpu.VMEM((BLOCK_FACES * mode, trace_width), jnp.float32),
-            pltpu.SemaphoreType.DMA((slots + 2,)),
+            pltpu.SemaphoreType.DMA((slots + 2 + inner_width * FACES // (BLOCK_FACES * trace_width),)),
             pltpu.SemaphoreType.DMA((1,)),
             pltpu.SemaphoreType.DMA((SWEEPS + 1,)),
         ],

time: 20.8 us -> 20.4 us (0.981)
  Pallas kernels: 19.3 us -> 18.9 us
    pallas_call x1, Pallas kernels: 18.4 us -> 18 us  [on_device(): pl.pallas_call(functools.partial(kernel, axis_sizes), out_shape=(out, out...]
where the time goes in v3:
time: 20.4 us; the launch traced here: 20.2 us
  Pallas kernels  18.9 us (93%)
  between operations  1.28 us (6%)
    pallas_call x1, Pallas kernels, on_device(): pl.pallas_call(functools.partial(kernel, axis_sizes), out_shape=(out, out...  18 us
    pallas_call x1, Pallas kernels, on_device(): pl.pallas_call(write_kernel, out_shape=(result, result), in_specs=[vmem,...  0.89 us

profile of v3, /device:TPU:0, one launch (start us, length us, event | category | flops | bytes accessed | tf_op | source)
XLA Modules:
  0.0 20.2 jit_solution(2191127164951207345)
XLA Ops:
  1.3 18.0 %condense_and_sweep.1 = (f32[768,128]{1,0:T(8,128)S(1)}, f32[768,128]{1,0:T(8,128)S(1)}) custom-call(bf16[4,768,768]{2,1,0:T(8,128)(2,1)} %bitcast.7, bf16[4,768,768]{2,1,0:T(8,128)(2,1)} %bitcast.8, bf16[768,768]{1,0:T(8,128)(2,1)} %bitcast.9, s32[1,1]{1,0:T(1,128)S(6)} %copy.8.counts, f32[768,128]{1,0:T(8,128)} %bitcast.10, f32[768,128]{1,0:T(8,128)} %bitcast.11), custom_call_target="tpu_custom_call" | custom-call | tf_op jit(solution)/shard_map/condense_and_sweep/pallas_call | solution.py:441
  19.3 0.9 %write_results.1 = (f32[768,128]{1,0:T(8,128)}, f32[768,128]{1,0:T(8,128)}) custom-call(f32[768,128]{1,0:T(8,128)S(1)} %get-tuple-element.6.traces, f32[768,128]{1,0:T(8,128)S(1)} %get-tuple-element.7.residual), custom_call_target="tpu_custom_call" | custom-call | tf_op jit(solution)/shard_map/write_results/pallas_call | solution.py:484

commit v4 on v3

--- a/solution.py
+++ b/solution.py
@@ -113,6 +113,9 @@
     def wait_for(place, sem):
         pltpu.make_async_copy(place, place, sem).wait()
 
+    def block_span(index):
+        return pl.ds(index * block, block)
+
     chunks = inner_width // block
     given_sem = in_sems.at[0]
     chunk_sems = [in_sems.at[1 + chunk] for chunk in range(chunks)]
@@ -130,7 +133,9 @@
         pltpu.make_async_copy(inverse.at[slot], inv.at[slot], slot_sems[slot]).start()
 
     def load_stiff():
-        pltpu.make_async_copy(stiffness, stiff, stiff_sem).start()
+        for index in range(blocks):
+            part = (block_span(index), pl.ds(index * block, trace_width - index * block))
+            pltpu.make_async_copy(stiffness.at[part], stiff.at[part], stiff_sem).start()
 
     load_slot(1)
 
@@ -200,9 +205,6 @@
     def face_span(face):
         return pl.ds(face * mode, mode)
 
-    def block_span(index):
-        return pl.ds(index * block, block)
-
     def block_rows(index):
         return slice(index * block, (index + 1) * block)
 
@@ -277,6 +279,9 @@
         if slot > 0:
             wait_slot(slot)
         product_of(0, slot)
+        if slot == MEET:
+            pl.semaphore_wait(barrier, partners)
+            send(0, range(LINKED))
         if slot == 0:
             wait_for(wide.at[pl.ds(0, trace_width - block), inner_span(0)], rest_sem)
             load_slot(3)
@@ -289,11 +294,8 @@
             traces[...] = start
             keep_parts(start)
             bound_t[...] = given[1].T
-        if slot == MEET:
-            pl.semaphore_wait(barrier, partners)
-            send(0, range(LINKED))
         if slot + 1 == slots:
-            wait_for(stiff, stiff_sem)
+            wait_for(stiff.at[pl.ds(0, (trace_width + block) // 2)], stiff_sem)
         condense_first(slot)
 
     linked_blocks = LINKED // BLOCK_FACES

time: 20.4 us -> 20.1 us (0.985)
    pallas_call x1, Pallas kernels: 18 us -> 17.8 us  [on_device(): pl.pallas_call(functools.partial(kernel, axis_sizes), out_shape=(out, out...]
where the time goes in v4:
time: 20.1 us; the launch traced here: 19.9 us
  Pallas kernels  18.7 us (93%)
  between operations  1.28 us (6%)
    pallas_call x1, Pallas kernels, on_device(): pl.pallas_call(functools.partial(kernel, axis_sizes), out_shape=(out, out...  17.8 us
    pallas_call x1, Pallas kernels, on_device(): pl.pallas_call(write_kernel, out_shape=(result, result), in_specs=[vmem,...  0.89 us

profile of v4, /device:TPU:0, one launch (start us, length us, event | category | flops | bytes accessed | tf_op | source)
XLA Modules:
  0.0 19.9 jit_solution(5234713825331954068)
XLA Ops:
  1.3 17.8 %condense_and_sweep.1 = (f32[768,128]{1,0:T(8,128)S(1)}, f32[768,128]{1,0:T(8,128)S(1)}) custom-call(bf16[4,768,768]{2,1,0:T(8,128)(2,1)} %bitcast.7, bf16[4,768,768]{2,1,0:T(8,128)(2,1)} %bitcast.8, bf16[768,768]{1,0:T(8,128)(2,1)} %bitcast.9, s32[1,1]{1,0:T(1,128)S(6)} %copy.8.counts, f32[768,128]{1,0:T(8,128)} %bitcast.10, f32[768,128]{1,0:T(8,128)} %bitcast.11), custom_call_target="tpu_custom_call" | custom-call | tf_op jit(solution)/shard_map/condense_and_sweep/pallas_call | solution.py:443
  19.0 0.9 %write_results.1 = (f32[768,128]{1,0:T(8,128)}, f32[768,128]{1,0:T(8,128)}) custom-call(f32[768,128]{1,0:T(8,128)S(1)} %get-tuple-element.6.traces, f32[768,128]{1,0:T(8,128)S(1)} %get-tuple-element.7.residual), custom_call_target="tpu_custom_call" | custom-call | tf_op jit(solution)/shard_map/write_results/pallas_call | solution.py:486

commit v5 on v4

--- a/solution.py
+++ b/solution.py
@@ -11,7 +11,7 @@
 FACES = 6
 LINKED = 4
 BLOCK_FACES = 2
-EARLY = 2
+EARLY = 3
 MEET = 0
 NW = 256
 
@@ -278,24 +278,24 @@
     for slot in range(slots):
         if slot > 0:
             wait_slot(slot)
+        if slot + 1 == slots:
+            wait_for(stiff.at[pl.ds(0, (trace_width + block) // 2)], stiff_sem)
         product_of(0, slot)
         if slot == MEET:
             pl.semaphore_wait(barrier, partners)
             send(0, range(LINKED))
         if slot == 0:
             wait_for(wide.at[pl.ds(0, trace_width - block), inner_span(0)], rest_sem)
+            wait_for(given, given_sem)
             load_slot(3)
             load_stiff()
         if slot < EARLY:
             product_of(1, slot)
         if slot == 0:
-            wait_for(given, given_sem)
             start = given[0].T
             traces[...] = start
             keep_parts(start)
             bound_t[...] = given[1].T
-        if slot + 1 == slots:
-            wait_for(stiff.at[pl.ds(0, (trace_width + block) // 2)], stiff_sem)
         condense_first(slot)
 
     linked_blocks = LINKED // BLOCK_FACES

time: 20.1 us -> 19.4 us (0.965)
  Pallas kernels: 18.7 us -> 17.9 us
    pallas_call x1, Pallas kernels: 17.8 us -> 17.1 us  [on_device(): pl.pallas_call(functools.partial(kernel, axis_sizes), out_shape=(out, out...]
where the time goes in v5:
time: 19.4 us; the launch traced here: 19.2 us
  Pallas kernels  17.9 us (92%)
  between operations  1.28 us (7%)
    pallas_call x1, Pallas kernels, on_device(): pl.pallas_call(functools.partial(kernel, axis_sizes), out_shape=(out, out...  17.1 us
    pallas_call x1, Pallas kernels, on_device(): pl.pallas_call(write_kernel, out_shape=(result, result), in_specs=[vmem,...  0.89 us

profile of v5, /device:TPU:0, one launch (start us, length us, event | category | flops | bytes accessed | tf_op | source)
XLA Modules:
  0.0 19.2 jit_solution(14146857386936265560)
XLA Ops:
  1.3 17.1 %condense_and_sweep.1 = (f32[768,128]{1,0:T(8,128)S(1)}, f32[768,128]{1,0:T(8,128)S(1)}) custom-call(bf16[4,768,768]{2,1,0:T(8,128)(2,1)} %bitcast.7, bf16[4,768,768]{2,1,0:T(8,128)(2,1)} %bitcast.8, bf16[768,768]{1,0:T(8,128)(2,1)} %bitcast.9, s32[1,1]{1,0:T(1,128)S(6)} %copy.8.counts, f32[768,128]{1,0:T(8,128)} %bitcast.10, f32[768,128]{1,0:T(8,128)} %bitcast.11), custom_call_target="tpu_custom_call" | custom-call | tf_op jit(solution)/shard_map/condense_and_sweep/pallas_call | solution.py:443
  18.3 0.9 %write_results.1 = (f32[768,128]{1,0:T(8,128)}, f32[768,128]{1,0:T(8,128)}) custom-call(f32[768,128]{1,0:T(8,128)S(1)} %get-tuple-element.6.traces, f32[768,128]{1,0:T(8,128)S(1)} %get-tuple-element.7.residual), custom_call_target="tpu_custom_call" | custom-call | tf_op jit(solution)/shard_map/write_results/pallas_call | solution.py:486

commit v6 on v5

--- a/solution.py
+++ b/solution.py
@@ -336,7 +336,8 @@
             sent_half[0, face] = value[
                 :, (face % BLOCK_FACES) * mode : (face % BLOCK_FACES + 1) * mode
             ].astype(jnp.bfloat16)
-        send(2, faces)
+        if index + 1 == linked_blocks:
+            send(2, range(LINKED))
 
     wait_arrived(1)
     for face in range(FACES):

time: 19.4 us -> 19.3 us (level)
  no operation moved by 1% of the time
where the time goes in v6:
time: 19.3 us; the launch traced here: 19.1 us
  Pallas kernels  17.8 us (92%)
  between operations  1.28 us (7%)
    pallas_call x1, Pallas kernels, on_device(): pl.pallas_call(functools.partial(kernel, axis_sizes), out_shape=(out, out...  16.9 us
    pallas_call x1, Pallas kernels, on_device(): pl.pallas_call(write_kernel, out_shape=(result, result), in_specs=[vmem,...  0.89 us

profile of v6, /device:TPU:0, one launch (start us, length us, event | category | flops | bytes accessed | tf_op | source)
XLA Modules:
  0.0 19.1 jit_solution(14290408728865077874)
XLA Ops:
  1.3 16.9 %condense_and_sweep.1 = (f32[768,128]{1,0:T(8,128)S(1)}, f32[768,128]{1,0:T(8,128)S(1)}) custom-call(bf16[4,768,768]{2,1,0:T(8,128)(2,1)} %bitcast.7, bf16[4,768,768]{2,1,0:T(8,128)(2,1)} %bitcast.8, bf16[768,768]{1,0:T(8,128)(2,1)} %bitcast.9, s32[1,1]{1,0:T(1,128)S(6)} %copy.8.counts, f32[768,128]{1,0:T(8,128)} %bitcast.10, f32[768,128]{1,0:T(8,128)} %bitcast.11), custom_call_target="tpu_custom_call" | custom-call | tf_op jit(solution)/shard_map/condense_and_sweep/pallas_call | solution.py:444
  18.2 0.9 %write_results.1 = (f32[768,128]{1,0:T(8,128)}, f32[768,128]{1,0:T(8,128)}) custom-call(f32[768,128]{1,0:T(8,128)S(1)} %get-tuple-element.6.traces, f32[768,128]{1,0:T(8,128)S(1)} %get-tuple-element.7.residual), custom_call_target="tpu_custom_call" | custom-call | tf_op jit(solution)/shard_map/write_results/pallas_call | solution.py:487
